TPU v7x, 32 devices: a whole 2x2x4 slice. The times are simulated.
32 devices in a mesh: dom: 32 (over z, y, x, core).
Axes of the slice: x: 2, y: 2, z: 4, core: 2. Of those that a mesh axis runs over, the one named last changes fastest.
Arguments:
- displacement: float32 [8, 3, 65536], P(None, None, 'dom'), may hold values from -1.5 to 1.5
- adjoint_disp: float32 [8, 3, 65536], P(None, None, 'dom'), may hold values from -1.5 to 1.5
- pressure: float32 [8, 65536], P(None, 'dom'), may hold values from -3 to 3
- adjoint_pressure: float32 [8, 65536], P(None, 'dom'), may hold values from -3 to 3
- youngs: float32 [65536], P('dom'), may hold values from 0.5 to 2
- permeability: float32 [65536], P('dom'), may hold values from 0.3 to 3
- stiffness: float32 [24, 24], replicated
- send_nodes: int32 [8, 4096], P(None, 'dom'), may hold values from 0 to 2047
- send_cells: int32 [8, 4096], P(None, 'dom'), may hold values from 0 to 2047
- elem_nodes: int32 [8, 65536], P(None, 'dom'), may hold values from 0 to 3071, as said below
- inner_faces: int32 [2, 196608], P(None, 'dom'), may hold values from 0 to 2047
- cross_faces: int32 [2, 32768], P(None, 'dom'), may hold values from 0 to 2047, as said below
Outputs:
- grad_log_youngs: float32 [65536], P('dom')
- grad_log_perm: float32 [65536], P('dom')
Inputs may be any that keep to these rules, and one draw needn't show every extreme that they name: `send_cells`: entries refer to the partition's own cells; block j of partition c is read by partition c - o_j. `elem_nodes`: The first 1536 elements of each partition name only its own nodes; corner 0 of each of the last 512 is a ghost node. `cross_faces`: row 0 is an own cell; row 1 is j * 128 + g with d + o_j always on the axis. `inner_faces`: both rows name cells of the same partition.
All inputs are finite; a program needn't handle non-finite values.
Results may differ from a plain program's by a relative error of at most 0.0003.
Values sent between devices are 32-bit elements; how exact they have to be, the bound alone decides.
A program may use at most 192 MiB of HBM per device.

v0:
```python
import functools

import jax
import jax.numpy as jnp
from jax import lax
from jax.experimental import pallas as pl
from jax.experimental.pallas import tpu as pltpu
from jax.sharding import PartitionSpec as P

OFFSETS = (1, -1, 2, -2, 4, -4, 8, -8)
MESH = pl.DeviceIdType.MESH
LANES = 128
ROWS = 8
DOFS = 24
WIDE = 256


def pick(table, lo):
    return jnp.take_along_axis(table, lo, axis=1, mode="promise_in_bounds")


def spread(row):
    return jnp.broadcast_to(row, (ROWS, LANES))


def gather(tables, index, first, last):
    lo = index & (LANES - 1)
    hi = index >> 7
    out = None
    for block in range(first, last):
        got = [pick(table(block), lo) for table in tables]
        if out is None:
            out = got
        else:
            here = hi == block
            out = [jnp.where(here, new, old) for new, old in zip(got, out)]
    return out


def onehot(index):
    rows = lax.broadcasted_iota(jnp.int32, (WIDE, LANES), 0).astype(jnp.bfloat16)
    low = (index & (WIDE - 1)).astype(jnp.float32).astype(jnp.bfloat16)
    same = rows == jnp.broadcast_to(low, (WIDE, LANES))
    hot = jnp.where(same, jnp.bfloat16(1), jnp.bfloat16(0))
    return jnp.concatenate([hot, hot], axis=0)


def fill(parts, planes, blocks):
    for block in range(blocks):
        for number in range(0, len(planes), 2):
            both = jnp.concatenate(
                [
                    jnp.concatenate([plane(2 * block), plane(2 * block + 1)], axis=1)
                    for plane in planes[number : number + 2]
                ],
                axis=0,
            )
            top = both.astype(jnp.bfloat16)
            base = (block * len(planes) + number) * ROWS
            parts[base : base + 2 * ROWS, :WIDE] = top
            parts[base : base + 2 * ROWS, WIDE:] = (both - top.astype(jnp.float32)).astype(
                jnp.bfloat16
            )


def multiply(parts, indices, planes, blocks):
    right = jnp.concatenate([onehot(index) for index in indices], axis=1)
    got = jnp.dot(parts[...], right, preferred_element_type=jnp.float32)
    answers = []
    for number, index in enumerate(indices):
        hi = spread(index) >> 8
        mine = got[:, number * LANES : (number + 1) * LANES]
        out = [mine[plane * ROWS : (plane + 1) * ROWS] for plane in range(planes)]
        for block in range(1, blocks):
            here = hi == block
            for plane in range(planes):
                base = (block * planes + plane) * ROWS
                out[plane] = jnp.where(here, mine[base : base + ROWS], out[plane])
        answers.append(out)
    return answers


def scatter(terms, index, height):
    sub_hi = lax.broadcasted_iota(jnp.int32, (height, LANES), 0)
    sub_lo = lax.broadcasted_iota(jnp.int32, (LANES, LANES), 0).astype(jnp.bfloat16)
    left, right = [], []
    for term, where in zip(terms, index):
        top = term.astype(jnp.bfloat16).astype(jnp.float32)
        rest = term - top
        middle = rest.astype(jnp.bfloat16).astype(jnp.float32)
        low = rest - middle
        hi = where >> 7
        lo = (where & (LANES - 1)).astype(jnp.float32)
        for row in range(ROWS):
            cut = slice(row, row + 1)
            mask = jnp.broadcast_to(hi[cut], (height, LANES)) == sub_hi
            parts = [
                jnp.where(mask, jnp.broadcast_to(part[cut], (height, LANES)), 0.0)
                for part in (top, middle, low)
            ]
            left.append(jnp.concatenate(parts, axis=0).astype(jnp.bfloat16))
            same = jnp.broadcast_to(lo[cut].astype(jnp.bfloat16), (LANES, LANES)) == sub_lo
            right.append(jnp.where(same, jnp.bfloat16(1), jnp.bfloat16(0)))
    sums = lax.dot_general(
        jnp.concatenate(left, axis=1),
        jnp.concatenate(right, axis=1),
        (((1,), (1,)), ((), ())),
        preferred_element_type=jnp.float32,
    )
    return sums[:height] + sums[height : 2 * height] + sums[2 * height :]


def face_terms(product, perm_a, perm_b):
    total = perm_a + perm_b
    common = 2.0 * perm_a * perm_b * product / (total * total)
    return common * perm_b, common * perm_a


def kernel(
    count,
    disp,
    adj,
    press,
    adjpress,
    youngs,
    perm,
    stiff,
    send_nodes,
    send_cells,
    elem,
    inner,
    cross,
    out_young,
    out_perm,
    parts,
    cell_parts,
    permtab,
    outbox,
    ghost,
    back,
    returned,
    forward,
    adjoint,
    kron,
    strain,
    face_a,
    face_b,
    send_sem,
    recv_sem,
    back_send,
    back_recv,
):
    me = lax.axis_index("dom")
    slots = len(OFFSETS)
    node_blocks = disp.shape[2] // LANES
    cell_blocks = perm.shape[0]
    elem_blocks = elem.shape[1] // LANES
    edge_blocks = elem_blocks // 4
    inner_rows = inner.shape[1] // LANES
    cross_rows = cross.shape[1] // LANES

    def device(steps):
        return lax.rem(me + steps + count, count)

    barrier = pltpu.get_barrier_semaphore()
    for offset in OFFSETS:
        pl.semaphore_signal(barrier, inc=1, device_id=(device(offset),), device_id_type=MESH)

    for block in range(cell_blocks):
        permtab[block] = spread(perm[block : block + 1, :])
    for row in range(inner_rows):
        cut = slice(row * LANES, (row + 1) * LANES)
        face_a[row : row + 1, :] = inner[0:1, cut]
        face_b[row : row + 1, :] = inner[1:2, cut]
    for row in range(cross_rows):
        cut = slice(row * LANES, (row + 1) * LANES)
        face_a[inner_rows + row : inner_rows + row + 1, :] = cross[0:1, cut]
        face_b[inner_rows + row : inner_rows + row + 1, :] = cross[1:2, cut]

    def plane(number):
        source, comp = (disp, number) if number < 3 else (adj, number - 3)
        return lambda block: source[comp, :, block * LANES : (block + 1) * LANES]

    def cells(source):
        return lambda block: source[:, block * LANES : (block + 1) * LANES]

    planes = [plane(number) for number in range(6)]
    cell_planes = [cells(press), cells(adjpress)]
    perm_plane = [lambda block: permtab[block]]

    side = DOFS * ROWS
    tall = lax.broadcasted_iota(jnp.int32, (side, DOFS), 0) // ROWS
    unknown = lax.broadcasted_iota(jnp.int32, (side, DOFS), 1)
    repeat = jnp.where(tall == unknown, 1.0, 0.0).astype(jnp.bfloat16)
    row_step = lax.broadcasted_iota(jnp.int32, (side, 2 * side), 0) & (ROWS - 1)
    twice = jnp.concatenate([repeat, repeat], axis=0)
    column_step = lax.broadcasted_iota(jnp.int32, (side, 2 * side), 1) & (ROWS - 1)
    whole = stiff[...]
    top = whole.astype(jnp.bfloat16)
    for number, part in enumerate((top, (whole - top.astype(jnp.float32)).astype(jnp.bfloat16))):
        rows = jnp.dot(repeat, part, preferred_element_type=jnp.float32).astype(jnp.bfloat16)
        full = lax.dot_general(
            rows, twice, (((1,), (1,)), ((), ())), preferred_element_type=jnp.float32
        )
        kron[number] = jnp.where(row_step == column_step, full, 0.0).astype(jnp.bfloat16)

    fill(parts, planes, node_blocks // 2)
    fill(cell_parts, cell_planes, cell_blocks // 2)
    for pair in range(0, slots, 2):
        rows = [send_nodes[slot : slot + 1, :] for slot in (pair, pair + 1)]
        nodes = multiply(parts, rows, 6, node_blocks // 2)
        for slot in (pair, pair + 1):
            where = spread(send_cells[slot : slot + 1, :])
            values = gather(cell_planes, where, 0, cell_blocks)
            for number, value in enumerate(nodes[slot - pair] + values):
                outbox[slot, number] = value
    sent_perm = gather(perm_plane, send_cells[...], 0, cell_blocks)[0]
    for slot in range(slots):
        outbox[slot, 8] = spread(sent_perm[slot : slot + 1, :])

    pl.semaphore_wait(barrier, slots)
    copies = []
    for slot, offset in enumerate(OFFSETS):
        copies.append(
            pltpu.make_async_remote_copy(
                src_ref=outbox.at[slot],
                dst_ref=ghost.at[slot],
                send_sem=send_sem.at[slot],
                recv_sem=recv_sem.at[slot],
                device_id=(device(-offset),),
                device_id_type=MESH,
            )
        )
        copies[-1].start()

    out_perm[...] = jnp.zeros(out_perm.shape, jnp.float32)

    def inner_faces(step, carry):
        base = pl.multiple_of(step * ROWS, ROWS)
        where_a = face_a[pl.ds(base, ROWS), :]
        where_b = face_b[pl.ds(base, ROWS), :]
        products = []
        others = [where_b[row : row + 1] for row in range(ROWS)]
        others = multiply(cell_parts, others, 2, cell_blocks // 2)
        for row in range(ROWS):
            pa, qa = gather(cell_planes, spread(where_a[row : row + 1]), 0, cell_blocks)
            pb, qb = others[row]
            products.append(jnp.sum((pa - pb) * (qa - qb), axis=0, keepdims=True))
        product = jnp.concatenate(products, axis=0)
        perm_a = gather(perm_plane, where_a, 0, cell_blocks)[0]
        perm_b = gather(perm_plane, where_b, 0, cell_blocks)[0]
        term_a, term_b = face_terms(product, perm_a, perm_b)
        out_perm[...] += scatter([term_a, term_b], [where_a, where_b], cell_blocks)
        return carry

    lax.fori_loop(0, inner_rows // ROWS, inner_faces, 0)

    def keep(lanes, values, corner):
        for comp in range(3):
            base = (comp * 8 + corner) * ROWS
            near = slice(base, base + 2 * ROWS)
            both = jnp.concatenate([value[comp] for value in values], axis=0)
            top = both.astype(jnp.bfloat16)
            low = (both - top.astype(jnp.float32)).astype(jnp.bfloat16)
            forward[near, lanes] = top
            forward[DOFS * ROWS + base : DOFS * ROWS + base + 2 * ROWS, lanes] = low
            adjoint[near, lanes] = jnp.concatenate([value[3 + comp] for value in values], axis=0)

    def inner_elements(step, carry):
        lanes = pl.ds(pl.multiple_of(step * LANES, LANES), LANES)
        for corner in range(0, 8, 2):
            rows = [elem[one : one + 1, lanes] for one in (corner, corner + 1)]
            if corner < 6:
                values = multiply(parts, rows, 6, node_blocks // 2)
            else:
                values = [gather(planes, spread(row), 0, node_blocks) for row in rows]
            keep(lanes, values, corner)
        return carry

    lax.fori_loop(0, elem_blocks - edge_blocks, inner_elements, 0)

    for copy in copies:
        copy.wait_recv()

    def ghosts(number):
        return lambda block: ghost[block, number]

    where_a = face_a[inner_rows : inner_rows + cross_rows, :]
    where_b = face_b[inner_rows : inner_rows + cross_rows, :]
    products = []
    own = [where_a[row : row + 1] for row in range(cross_rows)]
    own = multiply(cell_parts, own, 2, cell_blocks // 2)
    for row in range(cross_rows):
        pa, qa = own[row]
        pb, qb = gather([ghosts(6), ghosts(7)], spread(where_b[row : row + 1]), 0, slots)
        products.append(jnp.sum((pa - pb) * (qa - qb), axis=0, keepdims=True))
    product = jnp.concatenate(products, axis=0)
    perm_a = gather(perm_plane, where_a, 0, cell_blocks)[0]
    perm_b = gather([ghosts(8)], where_b, 0, slots)[0]
    term_a, term_b = face_terms(product, perm_a, perm_b)
    owed = scatter([term_b], [where_b], slots)
    for slot in range(slots):
        back[slot] = owed[slot : slot + 1, :]
    out_perm[...] += scatter([term_a], [where_a], cell_blocks)
    backs = []
    for slot, offset in enumerate(OFFSETS):
        backs.append(
            pltpu.make_async_remote_copy(
                src_ref=back.at[slot],
                dst_ref=returned.at[slot],
                send_sem=back_send.at[slot],
                recv_sem=back_recv.at[slot],
                device_id=(device(offset),),
                device_id_type=MESH,
            )
        )
        backs[-1].start()

    far_planes = [ghosts(number) for number in range(6)]

    def edge_elements(step, carry):
        lanes = pl.ds(pl.multiple_of(step * LANES, LANES), LANES)
        for corner in range(0, 8, 2):
            values = []
            rows = [elem[one : one + 1, lanes] for one in (corner, corner + 1)]
            near = multiply(parts, rows, 6, node_blocks // 2)
            for row, mine in zip(rows, near):
                index = spread(row)
                far = gather(far_planes, index - node_blocks * LANES, 0, slots)
                inside = index < node_blocks * LANES
                values.append([jnp.where(inside, a, b) for a, b in zip(mine, far)])
            keep(lanes, values, corner)
        return carry

    lax.fori_loop(elem_blocks - edge_blocks, elem_blocks, edge_elements, 0)

    side = DOFS * ROWS
    wide = elem.shape[1] // 4

    for part in range(4):
        lanes = slice(part * wide, (part + 1) * wide)
        weighted = jnp.dot(kron[0], forward[:, lanes], preferred_element_type=jnp.float32)
        weighted += jnp.dot(
            kron[1, :, :side], forward[:side, lanes], preferred_element_type=jnp.float32
        )
        product = weighted * adjoint[:, lanes]
        sums = jnp.sum(product, axis=0, keepdims=True)
        for row in range(wide // LANES):
            spot = part * (wide // LANES) + row
            strain[spot : spot + 1, :] = sums[:, row * LANES : (row + 1) * LANES]
    out_young[...] = -youngs[...] * strain[...]

    for copy in backs:
        copy.wait_recv()
    arrived = jnp.concatenate([returned[slot] for slot in range(slots)], axis=0)
    out_perm[...] += scatter([arrived], [send_cells[...]], cell_blocks)
    for copy in copies + backs:
        copy.wait_send()


def on_device(count, *arguments):
    (disp, adj, press, adjpress, youngs, perm, stiff, nodes, cells, elem, inner, cross) = arguments
    blocks = youngs.shape[0] // LANES
    slots = len(OFFSETS)
    face_rows = (inner.shape[1] + cross.shape[1]) // LANES
    vmem = pl.BlockSpec(memory_space=pltpu.VMEM)
    tile = (ROWS, LANES)
    shape = jax.ShapeDtypeStruct((blocks, LANES), jnp.float32)
    young, flow = pl.pallas_call(
        functools.partial(kernel, count),
        out_shape=(shape, shape),
        in_specs=[vmem] * 12,
        out_specs=(vmem, vmem),
        scratch_shapes=[
            pltpu.VMEM((disp.shape[2] // WIDE * 6 * ROWS, 2 * WIDE), jnp.bfloat16),
            pltpu.VMEM((blocks // 2 * 2 * ROWS, 2 * WIDE), jnp.bfloat16),
            pltpu.VMEM((blocks,) + tile, jnp.float32),
            pltpu.VMEM((slots, 9) + tile, jnp.float32),
            pltpu.VMEM((slots, 9) + tile, jnp.float32),
            pltpu.VMEM((slots, 1, LANES), jnp.float32),
            pltpu.VMEM((slots, 1, LANES), jnp.float32),
            pltpu.VMEM((2 * DOFS * ROWS, elem.shape[1]), jnp.bfloat16),
            pltpu.VMEM((DOFS * ROWS, elem.shape[1]), jnp.float32),
            pltpu.VMEM((2, DOFS * ROWS, 2 * DOFS * ROWS), jnp.bfloat16),
            pltpu.VMEM((elem.shape[1] // LANES, LANES), jnp.float32),
            pltpu.VMEM((face_rows, LANES), jnp.int32),
            pltpu.VMEM((face_rows, LANES), jnp.int32),
            pltpu.SemaphoreType.DMA((slots,)),
            pltpu.SemaphoreType.DMA((slots,)),
            pltpu.SemaphoreType.DMA((slots,)),
            pltpu.SemaphoreType.DMA((slots,)),
        ],
        compiler_params=pltpu.CompilerParams(collective_id=0, has_side_effects=True),
    )(
        disp.transpose(1, 0, 2),
        adj.transpose(1, 0, 2),
        press,
        adjpress,
        youngs.reshape(blocks, LANES),
        perm.reshape(blocks, LANES),
        stiff,
        nodes,
        cells,
        elem,
        inner,
        cross,
    )
    return (young.reshape(-1), flow.reshape(-1))


def solution(mesh):
    in_specs = (
        P(None, None, "dom"),
        P(None, None, "dom"),
        P(None, "dom"),
        P(None, "dom"),
        P("dom"),
        P("dom"),
        P(),
        P(None, "dom"),
        P(None, "dom"),
        P(None, "dom"),
        P(None, "dom"),
        P(None, "dom"),
    )
    out_specs = (P("dom"), P("dom"))
    return jax.shard_map(
        functools.partial(on_device, mesh.shape["dom"]),
        mesh=mesh,
        in_specs=in_specs,
        out_specs=out_specs,
        check_vma=False,
    )
```

profile of v0, /device:TPU:0, one launch (start us, length us, event | category | flops | bytes accessed | tf_op | source)
XLA Modules:
  0.0 27.1 jit_solution(3614516550193037770)
XLA Ops:
  0.6 24.6 %shard_map.131 = (f32[16,128]{1,0:T(8,128)}, f32[16,128]{1,0:T(8,128)}) custom-call(f32[3,8,2048]{2,1,0:T(8,128)} %bitcast.6, f32[3,8,2048]{2,1,0:T(8,128)} %bitcast.7, f32[8,2048]{1,0:T(8,128)} %press.1, f32[8,2048]{1,0:T(8,128)} %adjpress.1, f32[16,128]{1,0:T(8,128)} %bitcast.8, f32[16,128]{1,0:T(8,128)} %bitcast.9, f32[24,24]{1,0:T(8,128)} %stiff.1, ...), custom_call_target="tpu_custom_call" | custom-call | tf_op jit(solution)/shard_map/pallas_call | solution.py:369
  25.2 0.0 copy-start
  25.2 1.3 %copy.16 = f32[2048]{0:T(1024)} copy(f32[2048]{0:T(1024)} %bitcast.11) | data formatting | bytes 16384
  26.5 0.0 copy-done
  26.5 0.6 %copy.17 = f32[2048]{0:T(1024)} copy(f32[2048]{0:T(1024)S(1)} %bitcast.10) | data formatting | bytes 16384
Async XLA Ops:
  25.2 1.3 %copy-start = (f32[16,128]{1,0:T(8,128)S(1)}, f32[16,128]{1,0:T(8,128)}, u32[]{:S(2)}) copy-start(f32[16,128]{1,0:T(8,128)} %get-tuple-element.5) | copy-start | bytes 24580
where the time goes:
time: 27.3 us; the launch traced here: 27.1 us
  Pallas kernels  24.6 us (90%)
  local copies, waits for them, and re-layouts  1.9 us (7%)
  between operations  0.65 us (2%)
    pallas_call x1, Pallas kernels, on_device(): pl.pallas_call(functools.partial(kernel, count), out_shape=(shape, shape)...  24.6 us
    unnamed x4, local copies, waits for them, and re-layouts  1.9 us

commit v1 on v0

--- a/solution.py
+++ b/solution.py
@@ -159,12 +159,21 @@
     inner_rows = inner.shape[1] // LANES
     cross_rows = cross.shape[1] // LANES
 
-    def device(steps):
-        return lax.rem(me + steps + count, count)
+    def on_axis(steps):
+        return (me + steps >= 0) & (me + steps < count)
 
     barrier = pltpu.get_barrier_semaphore()
-    for offset in OFFSETS:
-        pl.semaphore_signal(barrier, inc=1, device_id=(device(offset),), device_id_type=MESH)
+    around = 0
+    for slot, offset in enumerate(OFFSETS):
+        around += on_axis(offset).astype(jnp.int32)
+
+        @pl.when(on_axis(offset))
+        def _():
+            pl.semaphore_signal(barrier, inc=1, device_id=(me + offset,), device_id_type=MESH)
+
+        @pl.when(jnp.logical_not(on_axis(-offset)))
+        def _():
+            returned[slot] = jnp.zeros((1, LANES), jnp.float32)
 
     for block in range(cell_blocks):
         permtab[block] = spread(perm[block : block + 1, :])
@@ -218,20 +227,38 @@
     for slot in range(slots):
         outbox[slot, 8] = spread(sent_perm[slot : slot + 1, :])
 
-    pl.semaphore_wait(barrier, slots)
-    copies = []
-    for slot, offset in enumerate(OFFSETS):
-        copies.append(
-            pltpu.make_async_remote_copy(
-                src_ref=outbox.at[slot],
-                dst_ref=ghost.at[slot],
-                send_sem=send_sem.at[slot],
-                recv_sem=recv_sem.at[slot],
-                device_id=(device(-offset),),
-                device_id_type=MESH,
+    def exchange(source, target, sent, received, side):
+        return [
+            (
+                pltpu.make_async_remote_copy(
+                    src_ref=source.at[slot],
+                    dst_ref=target.at[slot],
+                    send_sem=sent.at[slot],
+                    recv_sem=received.at[slot],
+                    device_id=(me + side * offset,),
+                    device_id_type=MESH,
+                ),
+                on_axis(side * offset),
+                on_axis(-side * offset),
             )
-        )
-        copies[-1].start()
+            for slot, offset in enumerate(OFFSETS)
+        ]
+
+    def start(copies):
+        for copy, to, _ in copies:
+            pl.when(to)(copy.start)
+
+    def wait_recv(copies):
+        for copy, _, come in copies:
+            pl.when(come)(copy.wait_recv)
+
+    def wait_send(copies):
+        for copy, to, _ in copies:
+            pl.when(to)(copy.wait_send)
+
+    pl.semaphore_wait(barrier, around)
+    copies = exchange(outbox, ghost, send_sem, recv_sem, -1)
+    start(copies)
 
     out_perm[...] = jnp.zeros(out_perm.shape, jnp.float32)
 
@@ -279,8 +306,7 @@
 
     lax.fori_loop(0, elem_blocks - edge_blocks, inner_elements, 0)
 
-    for copy in copies:
-        copy.wait_recv()
+    wait_recv(copies)
 
     def ghosts(number):
         return lambda block: ghost[block, number]
@@ -302,19 +328,8 @@
     for slot in range(slots):
         back[slot] = owed[slot : slot + 1, :]
     out_perm[...] += scatter([term_a], [where_a], cell_blocks)
-    backs = []
-    for slot, offset in enumerate(OFFSETS):
-        backs.append(
-            pltpu.make_async_remote_copy(
-                src_ref=back.at[slot],
-                dst_ref=returned.at[slot],
-                send_sem=back_send.at[slot],
-                recv_sem=back_recv.at[slot],
-                device_id=(device(offset),),
-                device_id_type=MESH,
-            )
-        )
-        backs[-1].start()
+    backs = exchange(back, returned, back_send, back_recv, 1)
+    start(backs)
 
     far_planes = [ghosts(number) for number in range(6)]
 
@@ -350,12 +365,11 @@
             strain[spot : spot + 1, :] = sums[:, row * LANES : (row + 1) * LANES]
     out_young[...] = -youngs[...] * strain[...]
 
-    for copy in backs:
-        copy.wait_recv()
+    wait_recv(backs)
     arrived = jnp.concatenate([returned[slot] for slot in range(slots)], axis=0)
     out_perm[...] += scatter([arrived], [send_cells[...]], cell_blocks)
-    for copy in copies + backs:
-        copy.wait_send()
+    wait_send(copies)
+    wait_send(backs)
 
 
 def on_device(count, *arguments):

time: 27.3 us -> 24 us (0.88)
  Pallas kernels: 24.6 us -> 21.3 us
    pallas_call x1, Pallas kernels: 24.6 us -> 21.3 us  [on_device(): pl.pallas_call(functools.partial(kernel, count), out_shape=(shape, shape)...]
where the time goes in v1:
time: 24 us; the launch traced here: 23.9 us
  Pallas kernels  21.3 us (89%)
  local copies, waits for them, and re-layouts  1.9 us (8%)
  between operations  0.65 us (3%)
    pallas_call x1, Pallas kernels, on_device(): pl.pallas_call(functools.partial(kernel, count), out_shape=(shape, shape)...  21.3 us
    unnamed x4, local copies, waits for them, and re-layouts  1.9 us

profile of v1, /device:TPU:0, one launch (start us, length us, event | category | flops | bytes accessed | tf_op | source)
XLA Modules:
  0.0 23.9 jit_solution(13729344358148879979)
XLA Ops:
  0.6 21.3 %shard_map.131 = (f32[16,128]{1,0:T(8,128)}, f32[16,128]{1,0:T(8,128)}) custom-call(f32[3,8,2048]{2,1,0:T(8,128)} %bitcast.6, f32[3,8,2048]{2,1,0:T(8,128)} %bitcast.7, f32[8,2048]{1,0:T(8,128)} %press.1, f32[8,2048]{1,0:T(8,128)} %adjpress.1, f32[16,128]{1,0:T(8,128)} %bitcast.8, f32[16,128]{1,0:T(8,128)} %bitcast.9, f32[24,24]{1,0:T(8,128)} %stiff.1, ...), custom_call_target="tpu_custom_call" | custom-call | tf_op jit(solution)/shard_map/pallas_call | solution.py:383
  21.9 0.0 copy-start
  21.9 1.3 %copy.16 = f32[2048]{0:T(1024)} copy(f32[2048]{0:T(1024)} %bitcast.11) | data formatting | bytes 16384
  23.3 0.0 copy-done
  23.3 0.6 %copy.17 = f32[2048]{0:T(1024)} copy(f32[2048]{0:T(1024)S(1)} %bitcast.10) | data formatting | bytes 16384
Async XLA Ops:
  21.9 1.3 %copy-start = (f32[16,128]{1,0:T(8,128)S(1)}, f32[16,128]{1,0:T(8,128)}, u32[]{:S(2)}) copy-start(f32[16,128]{1,0:T(8,128)} %get-tuple-element.5) | copy-start | bytes 24580

commit v2 on v1

--- a/solution.py
+++ b/solution.py
@@ -175,17 +175,6 @@
         def _():
             returned[slot] = jnp.zeros((1, LANES), jnp.float32)
 
-    for block in range(cell_blocks):
-        permtab[block] = spread(perm[block : block + 1, :])
-    for row in range(inner_rows):
-        cut = slice(row * LANES, (row + 1) * LANES)
-        face_a[row : row + 1, :] = inner[0:1, cut]
-        face_b[row : row + 1, :] = inner[1:2, cut]
-    for row in range(cross_rows):
-        cut = slice(row * LANES, (row + 1) * LANES)
-        face_a[inner_rows + row : inner_rows + row + 1, :] = cross[0:1, cut]
-        face_b[inner_rows + row : inner_rows + row + 1, :] = cross[1:2, cut]
-
     def plane(number):
         source, comp = (disp, number) if number < 3 else (adj, number - 3)
         return lambda block: source[comp, :, block * LANES : (block + 1) * LANES]
@@ -197,22 +186,8 @@
     cell_planes = [cells(press), cells(adjpress)]
     perm_plane = [lambda block: permtab[block]]
 
-    side = DOFS * ROWS
-    tall = lax.broadcasted_iota(jnp.int32, (side, DOFS), 0) // ROWS
-    unknown = lax.broadcasted_iota(jnp.int32, (side, DOFS), 1)
-    repeat = jnp.where(tall == unknown, 1.0, 0.0).astype(jnp.bfloat16)
-    row_step = lax.broadcasted_iota(jnp.int32, (side, 2 * side), 0) & (ROWS - 1)
-    twice = jnp.concatenate([repeat, repeat], axis=0)
-    column_step = lax.broadcasted_iota(jnp.int32, (side, 2 * side), 1) & (ROWS - 1)
-    whole = stiff[...]
-    top = whole.astype(jnp.bfloat16)
-    for number, part in enumerate((top, (whole - top.astype(jnp.float32)).astype(jnp.bfloat16))):
-        rows = jnp.dot(repeat, part, preferred_element_type=jnp.float32).astype(jnp.bfloat16)
-        full = lax.dot_general(
-            rows, twice, (((1,), (1,)), ((), ())), preferred_element_type=jnp.float32
-        )
-        kron[number] = jnp.where(row_step == column_step, full, 0.0).astype(jnp.bfloat16)
-
+    for block in range(cell_blocks):
+        permtab[block] = spread(perm[block : block + 1, :])
     fill(parts, planes, node_blocks // 2)
     fill(cell_parts, cell_planes, cell_blocks // 2)
     for pair in range(0, slots, 2):
@@ -260,9 +235,34 @@
     copies = exchange(outbox, ghost, send_sem, recv_sem, -1)
     start(copies)
 
+    side = DOFS * ROWS
+    tall = lax.broadcasted_iota(jnp.int32, (side, DOFS), 0) // ROWS
+    unknown = lax.broadcasted_iota(jnp.int32, (side, DOFS), 1)
+    repeat = jnp.where(tall == unknown, 1.0, 0.0).astype(jnp.bfloat16)
+    row_step = lax.broadcasted_iota(jnp.int32, (side, 2 * side), 0) & (ROWS - 1)
+    twice = jnp.concatenate([repeat, repeat], axis=0)
+    column_step = lax.broadcasted_iota(jnp.int32, (side, 2 * side), 1) & (ROWS - 1)
+    whole = stiff[...]
+    top = whole.astype(jnp.bfloat16)
+    for number, part in enumerate((top, (whole - top.astype(jnp.float32)).astype(jnp.bfloat16))):
+        rows = jnp.dot(repeat, part, preferred_element_type=jnp.float32).astype(jnp.bfloat16)
+        full = lax.dot_general(
+            rows, twice, (((1,), (1,)), ((), ())), preferred_element_type=jnp.float32
+        )
+        kron[number] = jnp.where(row_step == column_step, full, 0.0).astype(jnp.bfloat16)
+
+    for row in range(inner_rows):
+        cut = slice(row * LANES, (row + 1) * LANES)
+        face_a[row : row + 1, :] = inner[0:1, cut]
+        face_b[row : row + 1, :] = inner[1:2, cut]
+    for row in range(cross_rows):
+        cut = slice(row * LANES, (row + 1) * LANES)
+        face_a[inner_rows + row : inner_rows + row + 1, :] = cross[0:1, cut]
+        face_b[inner_rows + row : inner_rows + row + 1, :] = cross[1:2, cut]
+
     out_perm[...] = jnp.zeros(out_perm.shape, jnp.float32)
 
-    def inner_faces(step, carry):
+    def inner_faces(step):
         base = pl.multiple_of(step * ROWS, ROWS)
         where_a = face_a[pl.ds(base, ROWS), :]
         where_b = face_b[pl.ds(base, ROWS), :]
@@ -276,11 +276,7 @@
         product = jnp.concatenate(products, axis=0)
         perm_a = gather(perm_plane, where_a, 0, cell_blocks)[0]
         perm_b = gather(perm_plane, where_b, 0, cell_blocks)[0]
-        term_a, term_b = face_terms(product, perm_a, perm_b)
-        out_perm[...] += scatter([term_a, term_b], [where_a, where_b], cell_blocks)
-        return carry
-
-    lax.fori_loop(0, inner_rows // ROWS, inner_faces, 0)
+        return face_terms(product, perm_a, perm_b), (where_a, where_b)
 
     def keep(lanes, values, corner):
         for comp in range(3):
@@ -293,7 +289,7 @@
             forward[DOFS * ROWS + base : DOFS * ROWS + base + 2 * ROWS, lanes] = low
             adjoint[near, lanes] = jnp.concatenate([value[3 + comp] for value in values], axis=0)
 
-    def inner_elements(step, carry):
+    def inner_elements(step):
         lanes = pl.ds(pl.multiple_of(step * LANES, LANES), LANES)
         for corner in range(0, 8, 2):
             rows = [elem[one : one + 1, lanes] for one in (corner, corner + 1)]
@@ -302,9 +298,35 @@
             else:
                 values = [gather(planes, spread(row), 0, node_blocks) for row in rows]
             keep(lanes, values, corner)
+
+    face_steps = inner_rows // ROWS
+    inner_blocks = elem_blocks - edge_blocks
+    each = inner_blocks // face_steps
+    assert face_steps * ROWS == inner_rows and each * face_steps == inner_blocks
+
+    def inner(step, carry):
+        terms, where = inner_faces(step)
+        for number in range(each):
+            inner_elements(step * each + number)
+            if number == 0:
+                out_perm[...] += scatter(terms, where, cell_blocks)
         return carry
 
-    lax.fori_loop(0, elem_blocks - edge_blocks, inner_elements, 0)
+    lax.fori_loop(0, face_steps, inner, 0)
+
+    wide = elem.shape[1] // 4
+
+    def strains(part):
+        lanes = slice(part * wide, (part + 1) * wide)
+        weighted = jnp.dot(kron[0], forward[:, lanes], preferred_element_type=jnp.float32)
+        weighted += jnp.dot(
+            kron[1, :, :side], forward[:side, lanes], preferred_element_type=jnp.float32
+        )
+        product = weighted * adjoint[:, lanes]
+        sums = jnp.sum(product, axis=0, keepdims=True)
+        for row in range(wide // LANES):
+            spot = part * (wide // LANES) + row
+            strain[spot : spot + 1, :] = sums[:, row * LANES : (row + 1) * LANES]
 
     wait_recv(copies)
 
@@ -324,16 +346,19 @@
     perm_a = gather(perm_plane, where_a, 0, cell_blocks)[0]
     perm_b = gather([ghosts(8)], where_b, 0, slots)[0]
     term_a, term_b = face_terms(product, perm_a, perm_b)
+    strains(0)
     owed = scatter([term_b], [where_b], slots)
     for slot in range(slots):
         back[slot] = owed[slot : slot + 1, :]
+    strains(1)
     out_perm[...] += scatter([term_a], [where_a], cell_blocks)
+    strains(2)
     backs = exchange(back, returned, back_send, back_recv, 1)
     start(backs)
 
     far_planes = [ghosts(number) for number in range(6)]
 
-    def edge_elements(step, carry):
+    def edge_elements(step):
         lanes = pl.ds(pl.multiple_of(step * LANES, LANES), LANES)
         for corner in range(0, 8, 2):
             values = []
@@ -345,29 +370,19 @@
                 inside = index < node_blocks * LANES
                 values.append([jnp.where(inside, a, b) for a, b in zip(mine, far)])
             keep(lanes, values, corner)
+
+    def edge(step, carry):
+        for number in range(2):
+            edge_elements(inner_blocks + 2 * step + number)
         return carry
 
-    lax.fori_loop(elem_blocks - edge_blocks, elem_blocks, edge_elements, 0)
-
-    side = DOFS * ROWS
-    wide = elem.shape[1] // 4
-
-    for part in range(4):
-        lanes = slice(part * wide, (part + 1) * wide)
-        weighted = jnp.dot(kron[0], forward[:, lanes], preferred_element_type=jnp.float32)
-        weighted += jnp.dot(
-            kron[1, :, :side], forward[:side, lanes], preferred_element_type=jnp.float32
-        )
-        product = weighted * adjoint[:, lanes]
-        sums = jnp.sum(product, axis=0, keepdims=True)
-        for row in range(wide // LANES):
-            spot = part * (wide // LANES) + row
-            strain[spot : spot + 1, :] = sums[:, row * LANES : (row + 1) * LANES]
-    out_young[...] = -youngs[...] * strain[...]
+    lax.fori_loop(0, edge_blocks // 2, edge, 0)
 
     wait_recv(backs)
     arrived = jnp.concatenate([returned[slot] for slot in range(slots)], axis=0)
+    strains(3)
     out_perm[...] += scatter([arrived], [send_cells[...]], cell_blocks)
+    out_young[...] = -youngs[...] * strain[...]
     wait_send(copies)
     wait_send(backs)
 

time: 24 us -> 20.4 us (0.85)
  Pallas kernels: 21.3 us -> 17.7 us
    pallas_call x1, Pallas kernels: 21.3 us -> 17.7 us  [on_device(): pl.pallas_call(functools.partial(kernel, count), out_shape=(shape, shape)...]
where the time goes in v2:
time: 20.4 us; the launch traced here: 20.3 us
  Pallas kernels  17.7 us (87%)
  local copies, waits for them, and re-layouts  1.9 us (9%)
  between operations  0.65 us (3%)
    pallas_call x1, Pallas kernels, on_device(): pl.pallas_call(functools.partial(kernel, count), out_shape=(shape, shape)...  17.7 us
    unnamed x4, local copies, waits for them, and re-layouts  1.9 us

profile of v2, /device:TPU:0, one launch (start us, length us, event | category | flops | bytes accessed | tf_op | source)
XLA Modules:
  0.0 20.3 jit_solution(702608799063134080)
XLA Ops:
  0.6 17.7 %shard_map.131 = (f32[16,128]{1,0:T(8,128)}, f32[16,128]{1,0:T(8,128)}) custom-call(f32[3,8,2048]{2,1,0:T(8,128)} %bitcast.6, f32[3,8,2048]{2,1,0:T(8,128)} %bitcast.7, f32[8,2048]{1,0:T(8,128)} %press.1, f32[8,2048]{1,0:T(8,128)} %adjpress.1, f32[16,128]{1,0:T(8,128)} %bitcast.8, f32[16,128]{1,0:T(8,128)} %bitcast.9, f32[24,24]{1,0:T(8,128)} %stiff.1, ...), custom_call_target="tpu_custom_call" | custom-call | tf_op jit(solution)/shard_map/pallas_call | solution.py:398
  18.3 0.0 copy-start
  18.4 1.3 %copy.16 = f32[2048]{0:T(1024)} copy(f32[2048]{0:T(1024)} %bitcast.11) | data formatting | bytes 16384
  19.7 0.0 copy-done
  19.7 0.6 %copy.17 = f32[2048]{0:T(1024)} copy(f32[2048]{0:T(1024)S(1)} %bitcast.10) | data formatting | bytes 16384
Async XLA Ops:
  18.3 1.3 %copy-start = (f32[16,128]{1,0:T(8,128)S(1)}, f32[16,128]{1,0:T(8,128)}, u32[]{:S(2)}) copy-start(f32[16,128]{1,0:T(8,128)} %get-tuple-element.5) | copy-start | bytes 24580

commit v3 on v2

--- a/solution.py
+++ b/solution.py
@@ -116,22 +116,13 @@
     return common * perm_b, common * perm_a
 
 
-def kernel(
-    count,
-    disp,
-    adj,
-    press,
-    adjpress,
-    youngs,
-    perm,
-    stiff,
-    send_nodes,
-    send_cells,
-    elem,
-    inner,
-    cross,
-    out_young,
-    out_perm,
+def kernel(count, first, second, *refs):
+    arguments, refs = refs[:12], refs[12:]
+    out, refs = refs[0], refs[1:]
+    out_young, out_perm = out.at[0], out.at[1]
+    (disp, adj, press, adjpress, youngs, perm), refs = refs[:6], refs[6:]
+    (stiff, send_nodes, send_cells, elem, inner, cross), refs = refs[:6], refs[6:]
+    (
     parts,
     cell_parts,
     permtab,
@@ -147,9 +138,18 @@
     face_b,
     send_sem,
     recv_sem,
-    back_send,
+ back_send,
     back_recv,
-):
+    load_sem,
+    ) = refs
+    held = (disp, adj, press, adjpress, youngs, perm)
+    held += (stiff, send_nodes, send_cells, elem, inner, cross)
+    loads = [
+        pltpu.make_async_copy(source, target, load_sem.at[number])
+        for number, (source, target) in enumerate(zip(arguments, held))
+    ]
+    for load in loads:
+        load.start()
     me = lax.axis_index("dom")
     slots = len(OFFSETS)
     node_blocks = disp.shape[2] // LANES
@@ -185,6 +185,9 @@
     planes = [plane(number) for number in range(6)]
     cell_planes = [cells(press), cells(adjpress)]
     perm_plane = [lambda block: permtab[block]]
+
+    for number in (2, 3, 7, 8, 5, 0, 1, 6, 9, 10, 11, 4):
+        loads[number].wait()
 
     for block in range(cell_blocks):
         permtab[block] = spread(perm[block : block + 1, :])
@@ -231,10 +234,6 @@
         for copy, to, _ in copies:
             pl.when(to)(copy.wait_send)
 
-    pl.semaphore_wait(barrier, around)
-    copies = exchange(outbox, ghost, send_sem, recv_sem, -1)
-    start(copies)
-
     side = DOFS * ROWS
     tall = lax.broadcasted_iota(jnp.int32, (side, DOFS), 0) // ROWS
     unknown = lax.broadcasted_iota(jnp.int32, (side, DOFS), 1)
@@ -312,7 +311,13 @@
                 out_perm[...] += scatter(terms, where, cell_blocks)
         return carry
 
-    lax.fori_loop(0, face_steps, inner, 0)
+    lax.fori_loop(0, first, inner, 0)
+
+    pl.semaphore_wait(barrier, around)
+    copies = exchange(outbox, ghost, send_sem, recv_sem, -1)
+    start(copies)
+
+    lax.fori_loop(first, second, inner, 0)
 
     wide = elem.shape[1] // 4
 
@@ -352,9 +357,10 @@
         back[slot] = owed[slot : slot + 1, :]
     strains(1)
     out_perm[...] += scatter([term_a], [where_a], cell_blocks)
-    strains(2)
     backs = exchange(back, returned, back_send, back_recv, 1)
     start(backs)
+
+    lax.fori_loop(second, face_steps, inner, 0)
 
     far_planes = [ghosts(number) for number in range(6)]
 
@@ -380,11 +386,23 @@
 
     wait_recv(backs)
     arrived = jnp.concatenate([returned[slot] for slot in range(slots)], axis=0)
+    strains(2)
     strains(3)
     out_perm[...] += scatter([arrived], [send_cells[...]], cell_blocks)
     out_young[...] = -youngs[...] * strain[...]
     wait_send(copies)
     wait_send(backs)
+
+
+def deliver(both, young, flow, sem):
+    copies = [
+        pltpu.make_async_copy(both.at[number], target, sem.at[number])
+        for number, target in enumerate((young, flow))
+    ]
+    for copy in copies:
+        copy.start()
+    for copy in copies:
+        copy.wait()
 
 
 def on_device(count, *arguments):
@@ -395,12 +413,27 @@
     vmem = pl.BlockSpec(memory_space=pltpu.VMEM)
     tile = (ROWS, LANES)
     shape = jax.ShapeDtypeStruct((blocks, LANES), jnp.float32)
-    young, flow = pl.pallas_call(
-        functools.partial(kernel, count),
-        out_shape=(shape, shape),
-        in_specs=[vmem] * 12,
-        out_specs=(vmem, vmem),
-        scratch_shapes=[
+    operands = (
+        disp.transpose(1, 0, 2),
+        adj.transpose(1, 0, 2),
+        press,
+        adjpress,
+        youngs.reshape(blocks, LANES),
+        perm.reshape(blocks, LANES),
+        stiff,
+        nodes,
+        cells,
+        elem,
+        inner,
+        cross,
+    )
+    both = pl.pallas_call(
+        functools.partial(kernel, count, 1, 5),
+        out_shape=pltpu.VMEM((2, blocks, LANES), jnp.float32),
+        in_specs=[pl.BlockSpec(memory_space=pltpu.HBM)] * 12,
+        out_specs=vmem,
+        scratch_shapes=[pltpu.VMEM(one.shape, one.dtype) for one in operands]
+        + [
             pltpu.VMEM((disp.shape[2] // WIDE * 6 * ROWS, 2 * WIDE), jnp.bfloat16),
             pltpu.VMEM((blocks // 2 * 2 * ROWS, 2 * WIDE), jnp.bfloat16),
             pltpu.VMEM((blocks,) + tile, jnp.float32),
@@ -418,22 +451,22 @@
             pltpu.SemaphoreType.DMA((slots,)),
             pltpu.SemaphoreType.DMA((slots,)),
             pltpu.SemaphoreType.DMA((slots,)),
+            pltpu.SemaphoreType.DMA((len(operands),)),
         ],
-        compiler_params=pltpu.CompilerParams(collective_id=0, has_side_effects=True),
-    )(
-        disp.transpose(1, 0, 2),
-        adj.transpose(1, 0, 2),
-        press,
-        adjpress,
-        youngs.reshape(blocks, LANES),
-        perm.reshape(blocks, LANES),
-        stiff,
-        nodes,
-        cells,
-        elem,
-        inner,
-        cross,
-    )
+        compiler_params=pltpu.CompilerParams(
+            collective_id=0, has_side_effects=True),
+    )(*operands)
+    size = blocks * LANES
+    whole = jax.ShapeDtypeStruct((blocks, LANES), jnp.float32)
+    anywhere = pl.BlockSpec(memory_space=pl.ANY)
+    young, flow = pl.pallas_call(
+        deliver,
+        out_shape=(whole, whole),
+        in_specs=[vmem],
+        out_specs=(anywhere, anywhere),
+        scratch_shapes=[pltpu.SemaphoreType.DMA((2,))],
+        compiler_params=pltpu.CompilerParams(vmem_limit_bytes=2**20),
+    )(both)
     return (young.reshape(-1), flow.reshape(-1))
 
 

time: 20.4 us -> 16.1 us (0.79)
  Pallas kernels: 17.7 us -> 15.3 us
  local copies, waits for them, and re-layouts: 1.9 us -> 0 us
    pallas_call x1 -> x2, Pallas kernels: 17.7 us -> 15.3 us  [the longest x1 14.7 us: on_device(): pl.pallas_call(functools.partial(kernel, count, 1, 5), out_shape=pltpu.VM...]
    unnamed x4 -> x0, local copies, waits for them, and re-layouts: 1.9 us -> none
where the time goes in v3:
time: 16.1 us; the launch traced here: 15.9 us
  Pallas kernels  15.3 us (95%)
  between operations  0.64 us (4%)
    pallas_call x1, Pallas kernels, on_device(): pl.pallas_call(functools.partial(kernel, count, 1, 5), out_shape=pltpu.VM...  14.7 us
    pallas_call x1, Pallas kernels, on_device(): pl.pallas_call(deliver, out_shape=(whole, whole), in_specs=[vmem], out_sp...  0.62 us

profile of v3, /device:TPU:0, one launch (start us, length us, event | category | flops | bytes accessed | tf_op | source)
XLA Modules:
  0.0 15.9 jit_solution(15175942739988604015)
XLA Ops:
  0.6 14.7 %shard_map.131.both = f32[2,16,128]{2,1,0:T(8,128)S(1)} custom-call(f32[3,8,2048]{2,1,0:T(8,128)} %bitcast.6, f32[3,8,2048]{2,1,0:T(8,128)} %bitcast.7, f32[8,2048]{1,0:T(8,128)} %refs_2_.1, f32[8,2048]{1,0:T(8,128)} %refs_3_.1, f32[16,128]{1,0:T(8,128)} %bitcast.8, f32[16,128]{1,0:T(8,128)} %bitcast.9, f32[24,24]{1,0:T(8,128)} %refs_6_.1, ...), custom_call_target="tpu_custom_call" | custom-call | tf_op jit(solution)/shard_map/pallas_call | solution.py:430
  15.3 0.6 %shard_map.132 = (f32[16,128]{1,0:T(8,128)}, f32[16,128]{1,0:T(8,128)}) custom-call(f32[2,16,128]{2,1,0:T(8,128)S(1)} %shard_map.131.both), custom_call_target="tpu_custom_call" | custom-call | tf_op jit(solution)/shard_map/pallas_call | solution.py:462

commit v4 on v3

--- a/solution.py
+++ b/solution.py
@@ -116,7 +116,7 @@
     return common * perm_b, common * perm_a
 
 
-def kernel(count, first, second, *refs):
+def kernel(count, *refs):
     arguments, refs = refs[:12], refs[12:]
     out, refs = refs[0], refs[1:]
     out_young, out_perm = out.at[0], out.at[1]
@@ -126,8 +126,10 @@
     parts,
     cell_parts,
     permtab,
-    outbox,
-    ghost,
+    node_box,
+    cell_box,
+    ghost_nodes,
+    ghost_cells,
     back,
     returned,
     forward,
@@ -136,8 +138,10 @@
     strain,
     face_a,
     face_b,
-    send_sem,
-    recv_sem,
+    node_send,
+    node_recv,
+    cell_send,
+    cell_recv,
  back_send,
     back_recv,
     load_sem,
@@ -199,11 +203,13 @@
         for slot in (pair, pair + 1):
             where = spread(send_cells[slot : slot + 1, :])
             values = gather(cell_planes, where, 0, cell_blocks)
-            for number, value in enumerate(nodes[slot - pair] + values):
-                outbox[slot, number] = value
+            for number, value in enumerate(nodes[slot - pair]):
+                node_box[slot, number] = value
+            for number, value in enumerate(values):
+                cell_box[slot, number] = value
     sent_perm = gather(perm_plane, send_cells[...], 0, cell_blocks)[0]
     for slot in range(slots):
-        outbox[slot, 8] = spread(sent_perm[slot : slot + 1, :])
+        cell_box[slot, 2] = spread(sent_perm[slot : slot + 1, :])
 
     def exchange(source, target, sent, received, side):
         return [
@@ -298,24 +304,30 @@
                 values = [gather(planes, spread(row), 0, node_blocks) for row in rows]
             keep(lanes, values, corner)
 
-    face_steps = inner_rows // ROWS
+    face_steps = inner_rows // ROWS // 2
     inner_blocks = elem_blocks - edge_blocks
     each = inner_blocks // face_steps
-    assert face_steps * ROWS == inner_rows and each * face_steps == inner_blocks
+    assert 2 * face_steps * ROWS == inner_rows and each * face_steps == inner_blocks
 
     def inner(step, carry):
-        terms, where = inner_faces(step)
-        for number in range(each):
-            inner_elements(step * each + number)
-            if number == 0:
-                out_perm[...] += scatter(terms, where, cell_blocks)
+        for half in range(2):
+            terms, where = inner_faces(2 * step + half)
+            for number in range(each // 2):
+                inner_elements(step * each + half * (each // 2) + number)
+                if number == 0:
+                    out_perm[...] += scatter(terms, where, cell_blocks)
         return carry
 
+    early = jnp.logical_not(on_axis(-2))
+    first = jnp.where(early, 1, 0)
+    second = jnp.where(early, 3, 2)
     lax.fori_loop(0, first, inner, 0)
 
     pl.semaphore_wait(barrier, around)
-    copies = exchange(outbox, ghost, send_sem, recv_sem, -1)
-    start(copies)
+    cell_copies = exchange(cell_box, ghost_cells, cell_send, cell_recv, -1)
+    node_copies = exchange(node_box, ghost_nodes, node_send, node_recv, -1)
+    start(cell_copies)
+    start(node_copies)
 
     lax.fori_loop(first, second, inner, 0)
 
@@ -333,10 +345,10 @@
             spot = part * (wide // LANES) + row
             strain[spot : spot + 1, :] = sums[:, row * LANES : (row + 1) * LANES]
 
-    wait_recv(copies)
-
-    def ghosts(number):
-        return lambda block: ghost[block, number]
+    wait_recv(cell_copies)
+
+    def ghosts(source, number):
+        return lambda block: source[block, number]
 
     where_a = face_a[inner_rows : inner_rows + cross_rows, :]
     where_b = face_b[inner_rows : inner_rows + cross_rows, :]
@@ -345,11 +357,11 @@
     own = multiply(cell_parts, own, 2, cell_blocks // 2)
     for row in range(cross_rows):
         pa, qa = own[row]
-        pb, qb = gather([ghosts(6), ghosts(7)], spread(where_b[row : row + 1]), 0, slots)
+        pb, qb = gather([ghosts(ghost_cells, 0), ghosts(ghost_cells, 1)], spread(where_b[row : row + 1]), 0, slots)
         products.append(jnp.sum((pa - pb) * (qa - qb), axis=0, keepdims=True))
     product = jnp.concatenate(products, axis=0)
     perm_a = gather(perm_plane, where_a, 0, cell_blocks)[0]
-    perm_b = gather([ghosts(8)], where_b, 0, slots)[0]
+    perm_b = gather([ghosts(ghost_cells, 2)], where_b, 0, slots)[0]
     term_a, term_b = face_terms(product, perm_a, perm_b)
     strains(0)
     owed = scatter([term_b], [where_b], slots)
@@ -362,7 +374,8 @@
 
     lax.fori_loop(second, face_steps, inner, 0)
 
-    far_planes = [ghosts(number) for number in range(6)]
+    wait_recv(node_copies)
+    far_planes = [ghosts(ghost_nodes, number) for number in range(6)]
 
     def edge_elements(step):
         lanes = pl.ds(pl.multiple_of(step * LANES, LANES), LANES)
@@ -377,20 +390,16 @@
                 values.append([jnp.where(inside, a, b) for a, b in zip(mine, far)])
             keep(lanes, values, corner)
 
-    def edge(step, carry):
-        for number in range(2):
-            edge_elements(inner_blocks + 2 * step + number)
-        return carry
-
-    lax.fori_loop(0, edge_blocks // 2, edge, 0)
-
+    for number in range(edge_blocks):
+        edge_elements(inner_blocks + number)
     wait_recv(backs)
     arrived = jnp.concatenate([returned[slot] for slot in range(slots)], axis=0)
     strains(2)
     strains(3)
     out_perm[...] += scatter([arrived], [send_cells[...]], cell_blocks)
     out_young[...] = -youngs[...] * strain[...]
-    wait_send(copies)
+    wait_send(cell_copies)
+    wait_send(node_copies)
     wait_send(backs)
 
 
@@ -428,7 +437,7 @@
         cross,
     )
     both = pl.pallas_call(
-        functools.partial(kernel, count, 1, 5),
+        functools.partial(kernel, count),
         out_shape=pltpu.VMEM((2, blocks, LANES), jnp.float32),
         in_specs=[pl.BlockSpec(memory_space=pltpu.HBM)] * 12,
         out_specs=vmem,
@@ -437,8 +446,10 @@
             pltpu.VMEM((disp.shape[2] // WIDE * 6 * ROWS, 2 * WIDE), jnp.bfloat16),
             pltpu.VMEM((blocks // 2 * 2 * ROWS, 2 * WIDE), jnp.bfloat16),
             pltpu.VMEM((blocks,) + tile, jnp.float32),
-            pltpu.VMEM((slots, 9) + tile, jnp.float32),
-            pltpu.VMEM((slots, 9) + tile, jnp.float32),
+            pltpu.VMEM((slots, 6) + tile, jnp.float32),
+            pltpu.VMEM((slots, 3) + tile, jnp.float32),
+            pltpu.VMEM((slots, 6) + tile, jnp.float32),
+            pltpu.VMEM((slots, 3) + tile, jnp.float32),
             pltpu.VMEM((slots, 1, LANES), jnp.float32),
             pltpu.VMEM((slots, 1, LANES), jnp.float32),
             pltpu.VMEM((2 * DOFS * ROWS, elem.shape[1]), jnp.bfloat16),
@@ -447,6 +458,8 @@
             pltpu.VMEM((elem.shape[1] // LANES, LANES), jnp.float32),
             pltpu.VMEM((face_rows, LANES), jnp.int32),
             pltpu.VMEM((face_rows, LANES), jnp.int32),
+            pltpu.SemaphoreType.DMA((slots,)),
+            pltpu.SemaphoreType.DMA((slots,)),
             pltpu.SemaphoreType.DMA((slots,)),
             pltpu.SemaphoreType.DMA((slots,)),
             pltpu.SemaphoreType.DMA((slots,)),

time: 16.1 us -> 14.6 us (0.907)
  Pallas kernels: 15.3 us -> 13.8 us
    pallas_call x1, Pallas kernels: 14.7 us -> 13.1 us  [on_device(): pl.pallas_call(functools.partial(kernel, count), out_shape=pltpu.VMEM((2,...]
where the time goes in v4:
time: 14.6 us; the launch traced here: 14.4 us
  Pallas kernels  13.8 us (95%)
  between operations  0.64 us (4%)
    pallas_call x1, Pallas kernels, on_device(): pl.pallas_call(functools.partial(kernel, count), out_shape=pltpu.VMEM((2,...  13.1 us
    pallas_call x1, Pallas kernels, on_device(): pl.pallas_call(deliver, out_shape=(whole, whole), in_specs=[vmem], out_sp...  0.62 us

profile of v4, /device:TPU:0, one launch (start us, length us, event | category | flops | bytes accessed | tf_op | source)
XLA Modules:
  0.0 14.4 jit_solution(14407470613914833324)
XLA Ops:
  0.6 13.1 %shard_map.131.both = f32[2,16,128]{2,1,0:T(8,128)S(1)} custom-call(f32[3,8,2048]{2,1,0:T(8,128)} %bitcast.6, f32[3,8,2048]{2,1,0:T(8,128)} %bitcast.7, f32[8,2048]{1,0:T(8,128)} %refs_2_.1, f32[8,2048]{1,0:T(8,128)} %refs_3_.1, f32[16,128]{1,0:T(8,128)} %bitcast.8, f32[16,128]{1,0:T(8,128)} %bitcast.9, f32[24,24]{1,0:T(8,128)} %refs_6_.1, ...), custom_call_target="tpu_custom_call" | custom-call | tf_op jit(solution)/shard_map/pallas_call | solution.py:439
  13.8 0.6 %shard_map.132 = (f32[16,128]{1,0:T(8,128)}, f32[16,128]{1,0:T(8,128)}) custom-call(f32[2,16,128]{2,1,0:T(8,128)S(1)} %shard_map.131.both), custom_call_target="tpu_custom_call" | custom-call | tf_op jit(solution)/shard_map/pallas_call | solution.py:475

commit v5 on v4

--- a/solution.py
+++ b/solution.py
@@ -13,6 +13,9 @@
 ROWS = 8
 DOFS = 24
 WIDE = 256
+EIGHT = jnp.float8_e4m3fn
+SCALE = 256.0
+STEPS = (1.0, 16.0, 512.0)
 
 
 def pick(table, lo):
@@ -43,6 +46,32 @@
     same = rows == jnp.broadcast_to(low, (WIDE, LANES))
     hot = jnp.where(same, jnp.bfloat16(1), jnp.bfloat16(0))
     return jnp.concatenate([hot, hot], axis=0)
+
+
+def weighted(index):
+    rows = lax.broadcasted_iota(jnp.int32, (WIDE, LANES), 0).astype(jnp.bfloat16)
+    low = (index & (WIDE - 1)).astype(jnp.float32).astype(jnp.bfloat16)
+    same = rows == jnp.broadcast_to(low, (WIDE, LANES))
+    hots = [jnp.where(same, jnp.bfloat16(SCALE / step), jnp.bfloat16(0)) for step in STEPS]
+    return jnp.concatenate([hot.astype(EIGHT) for hot in hots], axis=0)
+
+
+def fill_nodes(parts, planes, blocks):
+    height = 2 * len(planes) * ROWS
+    for block in range(0, blocks, 2):
+        rest = SCALE * jnp.concatenate(
+            [
+                jnp.concatenate([plane(2 * near), plane(2 * near + 1)], axis=1)
+                for near in (block, block + 1)
+                for plane in planes
+            ],
+            axis=0,
+        )
+        base = block // 2 * height
+        for number, step in enumerate(STEPS):
+            top = (step * rest).astype(EIGHT)
+            parts[base : base + height, number * WIDE : (number + 1) * WIDE] = top
+            rest = rest - top.astype(jnp.float32) * (1 / step)
 
 
 def fill(parts, planes, blocks):
@@ -63,8 +92,8 @@
             )
 
 
-def multiply(parts, indices, planes, blocks):
-    right = jnp.concatenate([onehot(index) for index in indices], axis=1)
+def multiply(parts, indices, planes, blocks, hot=onehot, scale=None):
+    right = jnp.concatenate([hot(index) for index in indices], axis=1)
     got = jnp.dot(parts[...], right, preferred_element_type=jnp.float32)
     answers = []
     for number, index in enumerate(indices):
@@ -76,6 +105,8 @@
             for plane in range(planes):
                 base = (block * planes + plane) * ROWS
                 out[plane] = jnp.where(here, mine[base : base + ROWS], out[plane])
+        if scale is not None:
+            out = [scale * one for one in out]
         answers.append(out)
     return answers
 
@@ -195,11 +226,15 @@
 
     for block in range(cell_blocks):
         permtab[block] = spread(perm[block : block + 1, :])
-    fill(parts, planes, node_blocks // 2)
+    fill_nodes(parts, planes, node_blocks // 2)
+
+    def nodes_at(rows):
+        return multiply(parts, rows, 6, node_blocks // 2, weighted, SCALE**-2)
+
     fill(cell_parts, cell_planes, cell_blocks // 2)
     for pair in range(0, slots, 2):
         rows = [send_nodes[slot : slot + 1, :] for slot in (pair, pair + 1)]
-        nodes = multiply(parts, rows, 6, node_blocks // 2)
+        nodes = nodes_at(rows)
         for slot in (pair, pair + 1):
             where = spread(send_cells[slot : slot + 1, :])
             values = gather(cell_planes, where, 0, cell_blocks)
@@ -299,7 +334,7 @@
         for corner in range(0, 8, 2):
             rows = [elem[one : one + 1, lanes] for one in (corner, corner + 1)]
             if corner < 6:
-                values = multiply(parts, rows, 6, node_blocks // 2)
+                values = nodes_at(rows)
             else:
                 values = [gather(planes, spread(row), 0, node_blocks) for row in rows]
             keep(lanes, values, corner)
@@ -382,7 +417,7 @@
         for corner in range(0, 8, 2):
             values = []
             rows = [elem[one : one + 1, lanes] for one in (corner, corner + 1)]
-            near = multiply(parts, rows, 6, node_blocks // 2)
+            near = nodes_at(rows)
             for row, mine in zip(rows, near):
                 index = spread(row)
                 far = gather(far_planes, index - node_blocks * LANES, 0, slots)
@@ -392,12 +427,12 @@
 
     for number in range(edge_blocks):
         edge_elements(inner_blocks + number)
+    strains(2)
+    strains(3)
+    out_young[...] = -youngs[...] * strain[...]
     wait_recv(backs)
     arrived = jnp.concatenate([returned[slot] for slot in range(slots)], axis=0)
-    strains(2)
-    strains(3)
     out_perm[...] += scatter([arrived], [send_cells[...]], cell_blocks)
-    out_young[...] = -youngs[...] * strain[...]
     wait_send(cell_copies)
     wait_send(node_copies)
     wait_send(backs)
@@ -443,7 +478,7 @@
         out_specs=vmem,
         scratch_shapes=[pltpu.VMEM(one.shape, one.dtype) for one in operands]
         + [
-            pltpu.VMEM((disp.shape[2] // WIDE * 6 * ROWS, 2 * WIDE), jnp.bfloat16),
+            pltpu.VMEM((disp.shape[2] // WIDE * 6 * ROWS, len(STEPS) * WIDE), EIGHT),
             pltpu.VMEM((blocks // 2 * 2 * ROWS, 2 * WIDE), jnp.bfloat16),
             pltpu.VMEM((blocks,) + tile, jnp.float32),
             pltpu.VMEM((slots, 6) + tile, jnp.float32),

time: 14.6 us -> 14.2 us (0.973)
  Pallas kernels: 13.8 us -> 13.4 us
    pallas_call x1, Pallas kernels: 13.1 us -> 12.7 us  [on_device(): pl.pallas_call(functools.partial(kernel, count), out_shape=pltpu.VMEM((2,...]
where the time goes in v5:
time: 14.2 us; the launch traced here: 14 us
  Pallas kernels  13.4 us (94%)
  between operations  0.64 us (5%)
    pallas_call x1, Pallas kernels, on_device(): pl.pallas_call(functools.partial(kernel, count), out_shape=pltpu.VMEM((2,...  12.7 us
    pallas_call x1, Pallas kernels, on_device(): pl.pallas_call(deliver, out_shape=(whole, whole), in_specs=[vmem], out_sp...  0.62 us

profile of v5, /device:TPU:0, one launch (start us, length us, event | category | flops | bytes accessed | tf_op | source)
XLA Modules:
  0.0 14.0 jit_solution(15782896940475026887)
XLA Ops:
  0.6 12.7 %shard_map.131.both = f32[2,16,128]{2,1,0:T(8,128)S(1)} custom-call(f32[3,8,2048]{2,1,0:T(8,128)} %bitcast.6, f32[3,8,2048]{2,1,0:T(8,128)} %bitcast.7, f32[8,2048]{1,0:T(8,128)} %refs_2_.1, f32[8,2048]{1,0:T(8,128)} %refs_3_.1, f32[16,128]{1,0:T(8,128)} %bitcast.8, f32[16,128]{1,0:T(8,128)} %bitcast.9, f32[24,24]{1,0:T(8,128)} %refs_6_.1, ...), custom_call_target="tpu_custom_call" | custom-call | tf_op jit(solution)/shard_map/pallas_call | solution.py:474
  13.4 0.6 %shard_map.132 = (f32[16,128]{1,0:T(8,128)}, f32[16,128]{1,0:T(8,128)}) custom-call(f32[2,16,128]{2,1,0:T(8,128)S(1)} %shard_map.131.both), custom_call_target="tpu_custom_call" | custom-call | tf_op jit(solution)/shard_map/pallas_call | solution.py:510
